TPU v7x, 32 devices: a whole 2x2x4 slice. The times are simulated.
32 devices in a mesh: rep: 2 (over y), seq: 4 (over z), tp: 4 (over x, core).
Axes of the slice: x: 2, y: 2, z: 4, core: 2. Of those that a mesh axis runs over, the one named last changes fastest.
Arguments:
- queries: bfloat16 [128, 64, 128], P(('rep', 'seq')), parts along dimension 0, may hold values from -9 to 9
- key_pages: bfloat16 [1024, 8, 64, 128], P(('rep', 'seq'), 'tp'), parts along dimension 0, may hold values from -4 to 4
- value_pages: bfloat16 [1024, 8, 64, 128], P(('rep', 'seq'), 'tp'), parts along dimension 0, may hold values from -6 to 6
- page_owner: int32 [128, 128], P('rep'), parts along dimension 0, may hold values from 0 to 3, as said below
- page_local: int32 [128, 128], P('rep'), parts along dimension 0, may hold values from 0 to 127, as said below
- seq_lengths: int32 [128], P('rep'), parts along dimension 0, may hold values from 1 to 8192, as said below
Outputs:
- attention: bfloat16 [128, 64, 128], P(('rep', 'seq'), 'tp'), parts along dimension 0
There are 2 independent parts, one for each index of `rep`. A program takes and returns all parts, laid end to end along the dimension named above; each array names one. Nothing has to cross between parts.
Inputs may be any that keep to these rules, and one draw needn't show every extreme that they name: The live slots (s * 64 < seq_lengths[b]) name pairs (page_owner, page_local) that are all different; the other slots hold 0. `page_local`: see page_owner. `seq_lengths`: one sequence has exactly 8192 tokens; the live slots of all sequences together number at most half of the 512 pages.
All inputs are finite; a program needn't handle non-finite values.
Results may differ from a plain program's by a relative error of at most 0.008.
Values may be sent and summed in bfloat16 or wider, within the bound.
No kernel may reach another device: no remote copies, remote signals or barrier semaphores. Data moves between devices by JAX's collectives and lax.ppermute only.
A program may use at most 64 MiB of HBM per device.

v0:
```python
import math

import jax
import jax.numpy as jnp
from jax import lax
from jax.sharding import PartitionSpec as P

HQ = 64
KVH = 8


score_shift = 8.0


def body(queries, key_pages, value_pages, page_owner, page_local, seq_lengths):
    seq_count = page_owner.shape[0]
    slot_count = page_owner.shape[1]
    pool_pages = key_pages.shape[0]
    kv_local = key_pages.shape[1]
    page_len = key_pages.shape[2]
    head_dim = key_pages.shape[3]
    group_size = HQ // KVH
    heads_local = kv_local * group_size
    seq_rank = lax.axis_index("seq")
    tp_rank = lax.axis_index("tp")
    slot_ids = jnp.arange(slot_count, dtype=jnp.int32)
    slot_fill = jnp.clip(seq_lengths[:, None] - slot_ids[None, :] * page_len, 0, page_len)
    owned = (slot_fill > 0) & (page_owner == seq_rank)
    pool_range = jnp.arange(pool_pages, dtype=jnp.int32)
    matches = ((page_local[:, :, None] == pool_range[None, None, :]) & owned[:, :, None]).astype(
        jnp.bfloat16
    )
    fill_weight = slot_fill.astype(jnp.bfloat16)
    fill_table = jnp.einsum("bsp,bs->bp", matches, fill_weight, preferred_element_type=jnp.float32)
    hit_table = jnp.sum(matches.astype(jnp.float32), axis=1)
    seq_weight = jnp.arange(seq_count, dtype=jnp.float32)
    page_seq = jnp.dot(seq_weight, hit_table, precision=lax.Precision.HIGHEST).astype(jnp.int32)
    page_fill = jnp.sum(fill_table, axis=0).astype(jnp.int32)
    local_heads = lax.dynamic_slice_in_dim(queries, tp_rank * heads_local, heads_local, 1)
    head_queries = lax.all_gather(local_heads, "seq", axis=0, tiled=True)
    query_flat = head_queries.reshape(seq_count, heads_local * head_dim)
    score_scale = 1.0 / math.sqrt(head_dim)
    seq_range = jnp.arange(seq_count, dtype=jnp.int32)
    count = page_seq.shape[0]
    selector = page_seq[:, None] == seq_range[None, :]
    picked = jnp.dot(
        selector.astype(jnp.bfloat16), query_flat, preferred_element_type=jnp.float32
    ).astype(jnp.bfloat16)
    picked = picked.reshape(count, kv_local, group_size, head_dim)
    scores = (
        jnp.einsum("pkgd,pktd->pkgt", picked, key_pages, preferred_element_type=jnp.float32)
        * score_scale
    )
    live_mask = jnp.arange(page_len, dtype=jnp.int32)[None, :] < page_fill[:, None]
    weight = jnp.where(live_mask[:, None, None, :], jnp.exp(scores - score_shift), 0.0)
    page_total = jnp.sum(weight, axis=-1)
    page_sum = jnp.einsum(
        "pkgt,pktd->pkgd",
        weight.astype(jnp.bfloat16),
        value_pages,
        preferred_element_type=jnp.float32,
    )
    spread = selector.astype(jnp.float32).T
    numerator = jnp.dot(
        spread, page_sum.reshape(count, heads_local * head_dim), precision=lax.Precision.HIGHEST
    )
    denominator = jnp.dot(
        spread, page_total.reshape(count, heads_local), precision=lax.Precision.HIGHEST
    )
    numerator, denominator = (numerator, denominator)
    own_rows = seq_count // lax.axis_size("seq")
    summed_num, summed_den = lax.psum((numerator, denominator), "seq")
    summed_num = lax.dynamic_slice_in_dim(summed_num, seq_rank * own_rows, own_rows, 0)
    summed_den = lax.dynamic_slice_in_dim(summed_den, seq_rank * own_rows, own_rows, 0)
    result = summed_num.reshape(own_rows, heads_local, head_dim) / summed_den[..., None]
    return result.astype(jnp.bfloat16)


def solution(mesh):
    placed = (
        P(("rep", "seq"), None, None),
        P(("rep", "seq"), "tp", None, None),
        P(("rep", "seq"), "tp", None, None),
        P("rep", None),
        P("rep", None),
        P("rep"),
    )
    return jax.shard_map(
        body, mesh=mesh, in_specs=placed, out_specs=P(("rep", "seq"), "tp", None), check_vma=False
    )
```

profile of v0, /device:TPU:0, one launch (start us, length us, event | category | flops | bytes accessed | tf_op | source)
XLA Modules:
  0.0 89.1 jit_solution(877653192962036179)
XLA Ops:
  6.5 0.0 copy-start
  6.5 0.0 all-reduce.2.cloned.1.call-start
  6.5 0.8 fusion.35
  7.3 0.8 fusion.34
  8.2 4.5 %convert_reduce_fusion = f32[64,128]{1,0:T(8,128)S(1)} fusion(s32[64,128]{1,0:T(8,128)} %param.10, pred[64,128]{1,0:T(8,128)(4,1)S(1)} %fusion.34), kind=kLoop, calls=%fused_computation | loop fusion | flops 5234688 | bytes 73728 | tf_op jit(solution)/shard_map/reduce_sum | solution.py:35
  12.7 3.1 %fusion.14 = s32[128]{0:T(128)S(1)} fusion(s32[64,128]{1,0:T(8,128)} %param.10, pred[64,128]{1,0:T(8,128)(4,1)S(1)} %fusion.34, bf16[64,128,1]{1,0,2:T(8,128)(2,1)S(1)} %fusion.35), kind=kOutput, calls=%fused_computation.16 | convolution fusion | flops 4194432 | bytes 57856 | tf_op jit(solution)/shard_map/bsp,bs->bp/dot_general | solution.py:34
  15.8 0.1 iota_compare_fusion.1
  15.9 0.1 fusion.10
  16.0 0.0 copy-done
  16.0 0.0 copy-start.1
  16.1 15.8 %all_gather.3 = bf16[64,16,128]{2,1,0:T(8,128)(2,1)S(1)} all-gather(bf16[16,16,128]{2,1,0:T(8,128)(2,1)S(1)} %constant_dynamic-slice_fusion.1), channel_id=1, replica_groups=mesh['rep'=2,'seq'=4,'tp'=4] {'seq'}, dimensions={0}, use_global_device_ids=true | all-gather | bytes 327680 | tf_op jit(solution)/shard_map/all_gather | solution.py:40
  31.9 0.3 fusion.9
  32.2 0.1 copy.11
  32.3 4.6 %fusion.38 = (f32[128,2,8]{2,1,0:T(2,128)S(1)}, bf16[128,2,8,64]{3,2,1,0:T(8,128)(2,1)S(1)}) fusion(bf16[128,2,8,128]{3,2,1,0:T(8,128)(2,1)S(1)} %bitcast.38, bf16[128,2,64,128]{3,2,1,0:T(8,128)(2,1)} %param.7, pred[128,64]{1,0:T(8,128)(4,1)S(1)} %iota_compare_fusion.1), kind=kOutput, calls=%fused_computation.45 | convolution fusion | flops 34207744 | bytes 4997120 | tf_op jit(solution)/shard_map/pkgd,pktd->pkgt/dot_general | solution.py:51
  37.0 0.0 copy-done.1
  37.0 1.2 %fusion.20 = f32[128,2,8,128]{3,2,1,0:T(8,128)S(1)} fusion(bf16[128,2,64,128]{3,2,1,0:T(8,128)(2,1)S(1)} %copy-done.1, bf16[128,2,8,64]{3,2,1,0:T(8,128)(2,1)S(1)} %get-tuple-element.6), kind=kOutput, calls=%fused_computation.20 | convolution fusion | flops 33554432 | bytes 5505024 | tf_op jit(solution)/shard_map/pkgt,pktd->pkgd/dot_general | solution.py:57
  38.2 1.7 %fusion.17 = f32[64,2048]{1,0:T(8,128)} fusion(f32[16,8,16,128]{3,2,1,0:T(8,128)S(1)} %bitcast.37, s32[128]{0:T(128)S(1)} %fusion.10), kind=kOutput, calls=%fused_computation.17 | convolution fusion | flops 201334784 | bytes 1573376 | tf_op jit(solution)/shard_map/dot_general | solution.py:64
  39.8 0.0 all-reduce.2.cloned.1.call-update
  39.8 0.1 copy.8
  39.9 0.3 fusion.26
  40.2 20.0 %psum.15 = f32[64,16]{1,0:T(8,128)S(1)} all-reduce(f32[64,16]{1,0:T(8,128)S(1)} %fusion.26), channel_id=1, replica_groups=mesh['rep'=2,'seq'=4,'tp'=4] {'seq'}, use_global_device_ids=true, to_apply=%region_3.4 | all-reduce | flops 1024 | bytes 8192 | tf_op jit(solution)/shard_map/psum | solution.py:72
  60.2 20.3 %all-reduce.2.cloned.1.call-done = f32[64,2048]{1,0:T(8,128)} async-done(((f32[64,2048]{1,0:T(8,128)}), f32[64,2048]{1,0:T(8,128)}) %all-reduce.2.cloned.1.call-update) | async-done | bytes 524304 | tf_op jit(solution)/shard_map/psum | solution.py:72
  80.6 0.9 %dynamic-slice_bitcast_fusion = f32[2,8,16,128]{3,1,2,0:T(8,128)S(1)} fusion(f32[64,2048]{1,0:T(8,128)} %all-reduce.2.cloned.1.call-done, s32[]{:T(128)S(6)} %select_n.13), kind=kLoop, calls=%fused_computation.26 | loop fusion | bytes 262148
  81.5 0.7 fusion.24
  (4 shorter events, 0.1 us)
Async XLA Ops:
  6.5 9.5 %copy-start = (bf16[16,64,128]{2,1,0:T(8,128)(2,1)S(1)}, bf16[16,64,128]{2,1,0:T(8,128)(2,1)}, u32[]{:S(2)}) copy-start(bf16[16,64,128]{2,1,0:T(8,128)(2,1)} %param.6) | copy-start | bytes 786436
  6.5 74.0 %all-reduce.2.cloned.1.call-start = ((), (), s32[]{:S(2)}) async-start(), calls=%async_computation | async-start | bytes 1048576 | tf_op jit(solution)/shard_map/psum | solution.py:72
  16.0 20.9 %copy-start.1 = (bf16[128,2,64,128]{3,2,1,0:T(8,128)(2,1)S(1)}, bf16[128,2,64,128]{3,2,1,0:T(8,128)(2,1)}, u32[]{:S(2)}) copy-start(bf16[128,2,64,128]{3,2,1,0:T(8,128)(2,1)} %param.8) | copy-start | bytes 12582916
Sparse Core Ops, SparseCore 0:
  40.0 40.5 all-reduce.1
where the time goes:
time: 89.6 us; the launch traced here: 89.1 us
  blocking collectives  35.8 us (40%)
  waiting for transfers between devices  20.3 us (23%)
  between operations  13.5 us (15%)
  matrix products  11.4 us (13%)
  other arithmetic  6.96 us (8%)
  local copies, waits for them, and re-layouts  1.15 us (1%)
    psum x1, waiting for transfers between devices, body(): summed_num, summed_den = lax.psum((numerator, denominator), 'seq')  20.3 us
    psum x1, blocking collectives, body(): summed_num, summed_den = lax.psum((numerator, denominator), 'seq')  20 us
    all_gather x1, blocking collectives, body(): head_queries = lax.all_gather(local_heads, 'seq', axis=0, tiled=True)  15.8 us
    dot_general x1, matrix products, body(): jnp.einsum('pkgd,pktd->pkgt', picked, key_pages, preferred_element_type=j...  4.63 us
    reduce_sum x1, other arithmetic, body(): hit_table = jnp.sum(matches.astype(jnp.float32), axis=1)  4.51 us
    dot_general x1, matrix products, body(): jnp.einsum('bsp,bs->bp', matches, fill_weight, preferred_element_type=jnp...  3.1 us
  transfers between devices with their start and end apart: 1, of which 1 were waited for; matrix products, arithmetic and copies ran while one was open for 0% of the time, Pallas kernels for 0%

commit v1 on v0

v1 whole, which is shorter than its diff:
```python
import functools
import math

import jax
import jax.numpy as jnp
from jax import lax
from jax.experimental import pallas as pl
from jax.experimental.pallas import tpu as pltpu
from jax.sharding import PartitionSpec as P

HQ = 64
KVH = 8
GROUP = 16

score_shift = 8.0
log2_e = math.log2(math.e)


def direct(n):
    return n <= 8


def block_slot(block, rank, n):
    if not direct(n):
        return block
    if n & (n - 1) == 0:
        return block ^ rank
    return lax.rem(block - rank + n, n)


def fetch_pairs(n, s):
    if n & (n - 1) == 0:
        return [(i ^ s, i) for i in range(n)]
    return [((i + s) % n, i) for i in range(n)]


def table_kernel(
    lens, owner, local, keys, values, pos_out, page_out, fill_out, count_out, keys_out, values_out,
    sems, *, n, page_len
):
    loads = [
        pltpu.make_async_copy(keys, keys_out, sems.at[0]),
        pltpu.make_async_copy(values, values_out, sems.at[1]),
    ]
    for load in loads:
        load.start()
    rank = lax.axis_index("seq")
    seqs = owner.shape[0]
    own = seqs // n

    def visit_seq(b, count):
        length = lens[b]
        slots = lax.shift_right_logical(length + (page_len - 1), page_len.bit_length() - 1)
        block = b // own
        pos = block_slot(block, rank, n) * own + (b - block * own)

        def visit_slot(s, count):
            pos_out[count] = pos
            page_out[count] = local[b, s]
            fill_out[count] = jnp.minimum(length - s * page_len, page_len)
            return count + (owner[b, s] == rank).astype(jnp.int32)

        return lax.fori_loop(0, slots, visit_slot, count)

    count = lax.fori_loop(0, seqs, visit_seq, jnp.int32(0))
    for u in range(GROUP):
        pos_out[count + u] = 0
        page_out[count + u] = 0
        fill_out[count + u] = 0
    count_out[0] = lax.div(count + (GROUP - 1), GROUP)
    for load in loads:
        load.wait()


def attend_kernel(pos_t, page_t, fill_t, count, *refs, n, parts, kv):
    queries = refs[:parts]
    keys, values = refs[parts], refs[parts + 1]
    outs = refs[parts + 2 : parts + 2 + n]
    query, acc, wsum = refs[parts + 2 + n :]
    own = acc.shape[0] // n
    heads, head_dim = acc.shape[1], acc.shape[2]
    page_len = keys.shape[2]
    step = acc.shape[0] // parts
    for s in range(parts):
        query[pl.ds(s * step, step)] = queries[s][...]
    acc[...] = jnp.zeros_like(acc)
    wsum[...] = jnp.zeros_like(wsum)
    width = kv * page_len
    scale = log2_e / math.sqrt(head_dim)
    lane = lax.broadcasted_iota(jnp.int32, (heads, width), 1)
    row = lax.broadcasted_iota(jnp.int32, (heads, width), 0)
    token = jnp.where(
        lane // page_len == row // (heads // kv), lane % page_len, jnp.int32(page_len)
    )

    def visit(g, _):
        base = g * GROUP
        where = [pos_t[base + u] for u in range(GROUP)]
        pages = [page_t[base + u] for u in range(GROUP)]
        scores = [
            lax.dot_general(
                query[where[u]],
                keys[pages[u]].reshape(width, head_dim),
                (((1,), (1,)), ((), ())),
                preferred_element_type=jnp.float32,
            )
            for u in range(GROUP)
        ]
        weights = [
            jnp.where(
                token < fill_t[base + u],
                jnp.exp2(scores[u] * scale - score_shift * log2_e),
                0.0,
            )
            for u in range(GROUP)
        ]
        sums = [
            jnp.dot(
                weights[u].astype(jnp.bfloat16),
                values[pages[u]].reshape(width, head_dim),
                preferred_element_type=jnp.float32,
            )
            for u in range(GROUP)
        ]
        for u in range(GROUP):
            acc[where[u]] += sums[u]
            wsum[where[u]] += weights[u]
        return 0

    lax.fori_loop(0, count[0], visit, 0)
    lanes = lax.broadcasted_iota(jnp.int32, (heads, head_dim), 1)
    half = head_dim // 2
    for s in range(n):
        total = jnp.zeros((heads, head_dim), jnp.float32)
        for i in range(own):
            column = jnp.sum(wsum[s * own + i], axis=-1, keepdims=True)
            high = column.astype(jnp.bfloat16).astype(jnp.float32)
            total = jnp.where(lanes == i, high, total)
            total = jnp.where(lanes == half + i, column - high, total)
        outs[s][pl.ds(0, own)] = acc[pl.ds(s * own, own)].astype(outs[s].dtype)
        outs[s][own] = total.astype(outs[s].dtype)


def merge_kernel(*refs, own):
    out = refs[-1]
    total = refs[0][own].astype(jnp.float32)
    for ref in refs[1:-1]:
        total += ref[own].astype(jnp.float32)
    half = total.shape[1] // 2
    total = 1.0 / (total[:, :half] + total[:, half:])
    for i in range(own):
        numerator = refs[0][i].astype(jnp.float32)
        for ref in refs[1:-1]:
            numerator += ref[i].astype(jnp.float32)
        out[i] = (numerator * total[:, i : i + 1]).astype(out.dtype)


def body(queries, key_pages, value_pages, page_owner, page_local, seq_lengths):
    seq_count = page_owner.shape[0]
    pool_pages, kv_local, page_len, head_dim = key_pages.shape
    heads = kv_local * (HQ // KVH)
    n = lax.axis_size("seq")
    own = seq_count // n
    tp_rank = lax.axis_index("tp")
    mine = lax.dynamic_slice_in_dim(queries, tp_rank * heads, heads, 1)
    if direct(n):
        parts = [mine] + [lax.ppermute(mine, "seq", fetch_pairs(n, s)) for s in range(1, n)]
    else:
        parts = [lax.all_gather(mine, "seq", axis=0, tiled=True)]
    smem = pl.BlockSpec(memory_space=pltpu.SMEM)
    vmem = pl.BlockSpec(memory_space=pltpu.VMEM)
    table = jax.ShapeDtypeStruct((pool_pages + GROUP + 1,), jnp.int32)
    hbm = pl.BlockSpec(memory_space=pltpu.HBM)
    *tables, keys, values = pl.pallas_call(
        functools.partial(table_kernel, n=n, page_len=page_len),
        out_shape=[
            table,
            table,
            table,
            jax.ShapeDtypeStruct((1,), jnp.int32),
            jax.ShapeDtypeStruct(key_pages.shape, key_pages.dtype),
            jax.ShapeDtypeStruct(value_pages.shape, value_pages.dtype),
        ],
        in_specs=[smem] * 3 + [hbm] * 2,
        out_specs=[smem] * 4 + [vmem] * 2,
        scratch_shapes=[pltpu.SemaphoreType.DMA((2,))],
        compiler_params=pltpu.CompilerParams(vmem_limit_bytes=1024 * 1024),
        name="tables",
    )(seq_lengths, page_owner, page_local, key_pages, value_pages)
    sent = jax.ShapeDtypeStruct((own + 1, heads, head_dim), jnp.bfloat16)
    kept = jax.ShapeDtypeStruct((own + 1, heads, head_dim), jnp.float32)
    if direct(n):
        shapes = [kept] + [sent] * (n - 1)
    else:
        shapes = [sent] * n
    partial = pl.pallas_call(
        functools.partial(attend_kernel, n=n, parts=len(parts), kv=kv_local),
        out_shape=shapes,
        in_specs=[smem] * 4 + [vmem] * (len(parts) + 2),
        out_specs=[vmem] * n,
        scratch_shapes=[
            pltpu.VMEM((seq_count, heads, head_dim), jnp.bfloat16),
            pltpu.VMEM((seq_count, heads, head_dim), jnp.float32),
            pltpu.VMEM((seq_count, heads, kv_local * page_len), jnp.float32),
        ],
        compiler_params=pltpu.CompilerParams(vmem_limit_bytes=8 * 1024 * 1024),
        name="attend",
    )(*tables, *parts, keys, values)
    if direct(n):
        pieces = [partial[0]]
        for s in range(1, n):
            pairs = [(b, a) for a, b in fetch_pairs(n, s)]
            pieces.append(lax.ppermute(partial[s], "seq", pairs))
    else:
        arrived = lax.all_to_all(jnp.stack(partial), "seq", 0, 0)
        pieces = [arrived[s] for s in range(n)]
    return pl.pallas_call(
        functools.partial(merge_kernel, own=own),
        out_shape=jax.ShapeDtypeStruct((own, heads, head_dim), jnp.bfloat16),
        in_specs=[vmem] * n,
        out_specs=vmem,
        compiler_params=pltpu.CompilerParams(vmem_limit_bytes=4 * 1024 * 1024),
        name="merge",
    )(*pieces)


def solution(mesh):
    placed = (
        P(("rep", "seq"), None, None),
        P(("rep", "seq"), "tp", None, None),
        P(("rep", "seq"), "tp", None, None),
        P("rep", None),
        P("rep", None),
        P("rep"),
    )
    return jax.shard_map(
        body, mesh=mesh, in_specs=placed, out_specs=P(("rep", "seq"), "tp", None), check_vma=False
    )
```

time: 89.6 us -> 34.3 us (0.38)
  blocking collectives: 35.8 us -> 0 us
  waiting for transfers between devices: 20.3 us -> 4.39 us
  between operations: 13.5 us -> 0.06 us
  matrix products: 11.4 us -> 0 us
  Pallas kernels: 0 us -> 11.4 us
  starting transfers between devices: 0.01 us -> 10.2 us
  other arithmetic: 6.96 us -> 0 us
  local copies, waits for them, and re-layouts: 1.15 us -> 7.5 us
    psum x1 -> x0, waiting for transfers between devices: 20.3 us -> none  [body(): summed_num, summed_den = lax.psum((numerator, denominator), 'seq')]
    psum x1 -> x0, blocking collectives: 20 us -> none  [body(): summed_num, summed_den = lax.psum((numerator, denominator), 'seq')]
    all_gather x1 -> x0, blocking collectives: 15.8 us -> none  [body(): head_queries = lax.all_gather(local_heads, 'seq', axis=0, tiled=True)]
    pallas_call x0 -> x3, Pallas kernels: none -> 11.4 us  [the longest x1 5.82 us: body(): pl.pallas_call(functools.partial(table_kernel, n=n, page_len=page_len), o...]
    dot_general x7 -> x0, matrix products: 11.4 us -> none  [the longest x1 4.63 us: body(): jnp.einsum('pkgd,pktd->pkgt', picked, key_pages, preferred_element_type=j...]
    ppermute x0 -> x6, starting transfers between devices: none -> 10.2 us  [the longest x3 5.78 us: body(): lax.ppermute(mine, 'seq', fetch_pairs(n, s))]
    unnamed x7 -> x12, local copies, waits for them, and re-layouts: 1.06 us -> 7.49 us
    reduce_sum x1 -> x0, other arithmetic: 4.51 us -> none  [body(): hit_table = jnp.sum(matches.astype(jnp.float32), axis=1)]
  transfers between devices with their start and end apart: 1 -> 6, of which waited for: 1 -> 1; matrix products, arithmetic and copies ran while one was open for 0% -> 0% of each run, Pallas kernels for 0% -> 17%
where the time goes in v1:
time: 34.3 us; the launch traced here: 33.6 us
  Pallas kernels  11.4 us (33%)
  starting transfers between devices  10.2 us (30%)
  local copies, waits for them, and re-layouts  7.5 us (22%)
  waiting for transfers between devices  4.39 us (13%)
    unnamed x12, local copies, waits for them, and re-layouts  7.49 us
    pallas_call x1, Pallas kernels, body(): pl.pallas_call(functools.partial(table_kernel, n=n, page_len=page_len), o...  5.82 us
    ppermute x3, starting transfers between devices, body(): lax.ppermute(mine, 'seq', fetch_pairs(n, s))  5.78 us
    pallas_call x1, Pallas kernels, body(): pl.pallas_call(functools.partial(attend_kernel, n=n, parts=len(parts), kv...  4.78 us
    ppermute x3, starting transfers between devices, body(): pieces.append(lax.ppermute(partial[s], 'seq', pairs))  4.44 us
    ppermute x3, waiting for transfers between devices, body(): pieces.append(lax.ppermute(partial[s], 'seq', pairs))  4.38 us
    pallas_call x1, Pallas kernels, body(): pl.pallas_call(functools.partial(merge_kernel, own=own), out_shape=jax.Sh...  0.84 us
  transfers between devices with their start and end apart: 6, of which 1 were waited for; matrix products, arithmetic and copies ran while one was open for 0% of the time, Pallas kernels for 17%

profile of v1, /device:TPU:0, one launch (start us, length us, event | category | flops | bytes accessed | tf_op | source)
XLA Modules:
  0.0 33.6 jit_solution(9125615397585853168)
XLA Ops:
  0.0 0.0 copy-start
  0.0 0.9 %copy-done = bf16[16,64,128]{2,1,0:T(8,128)(2,1)S(1)} copy-done((bf16[16,64,128]{2,1,0:T(8,128)(2,1)S(1)}, bf16[16,64,128]{2,1,0:T(8,128)(2,1)}, u32[]{:S(2)}) %copy-start) | copy-done | bytes 262168
  1.0 5.1 %collective-permute-start.2 = (bf16[16,16,128]{2,1,0:T(8,128)(2,1)S(1)}, bf16[16,16,128]{2,1,0:T(8,128)(2,1)S(1)}, u32[]{:S(2)}, u32[]{:S(2)}) collective-permute-start(bf16[16,16,128]{2,1,0:T(8,128)(2,1)S(1)} %constant_dynamic-slice_fusion.refs_0_), channel_id=1, source_target_pairs={{12,0},{8,4},{4,8},{0,12},{13,1},{9,5},{5,9},{1,13},{14,2},{10,6},... | collective-permute-start | bytes 196616 | tf_op jit(solution)/shard_map/ppermute | solution.py:167
  6.1 0.0 collective-permute-start.1
  6.1 0.6 %collective-permute-start = (bf16[16,16,128]{2,1,0:T(8,128)(2,1)S(1)}, bf16[16,16,128]{2,1,0:T(8,128)(2,1)S(1)}, u32[]{:S(2)}, u32[]{:S(2)}) collective-permute-start(bf16[16,16,128]{2,1,0:T(8,128)(2,1)S(1)} %constant_dynamic-slice_fusion.refs_0_), channel_id=1, source_target_pairs={{4,0},{0,4},{12,8},{8,12},{5,1},{1,5},{13,9},{9,13},{6,2},{2,6},{1... | collective-permute-start | bytes 196616 | tf_op jit(solution)/shard_map/ppermute | solution.py:167
  6.8 0.0 copy-start.1
  6.8 2.2 %copy-done.1 = bf16[128,2,64,128]{3,2,1,0:T(8,128)(2,1)S(1)} copy-done((bf16[128,2,64,128]{3,2,1,0:T(8,128)(2,1)S(1)}, bf16[128,2,64,128]{3,2,1,0:T(8,128)(2,1)}, u32[]{:S(2)}) %copy-start.1) | copy-done | bytes 4194328
  8.9 0.0 copy-start.2
  8.9 2.2 %copy-done.2 = bf16[128,2,64,128]{3,2,1,0:T(8,128)(2,1)S(1)} copy-done((bf16[128,2,64,128]{3,2,1,0:T(8,128)(2,1)S(1)}, bf16[128,2,64,128]{3,2,1,0:T(8,128)(2,1)}, u32[]{:S(2)}) %copy-start.2) | copy-done | bytes 4194328
  11.1 0.8 %copy-done.3 = s32[64,128]{1,0:T(8,128)S(1)} copy-done((s32[64,128]{1,0:T(8,128)S(1)}, s32[64,128]{1,0:T(8,128)}, u32[]{:S(2)}) %copy-start.3) | copy-done | bytes 32792
  11.9 0.8 %copy-done.4 = s32[64,128]{1,0:T(8,128)S(1)} copy-done((s32[64,128]{1,0:T(8,128)S(1)}, s32[64,128]{1,0:T(8,128)}, u32[]{:S(2)}) %copy-start.4) | copy-done | bytes 32792
  12.6 0.7 %copy-done.5 = s32[64]{0:T(128)S(1)} copy-done((s32[64]{0:T(128)S(1)}, s32[64]{0:T(128)}, u32[]{:S(2)}) %copy-start.5) | copy-done | bytes 280
  13.3 5.8 %tables.1 = (s32[145]{0:T(256)S(1)}, s32[145]{0:T(256)S(1)}, s32[145]{0:T(256)S(1)}, s32[1]{0:T(128)}, bf16[128,2,64,128]{3,2,1,0:T(8,128)(2,1)S(1)}, /*index=5*/bf16[128,2,64,128]{3,2,1,0:T(8,128)(2,1)S(1)}) custom-call(s32[64]{0:T(128)S(1)} %copy-done.5, s32[64,128]{1,0:T(8,128)S(1)} %copy-done.3, s32[64,128]{1,0:T(8,128)S(1)} %copy-done.4, ...), custom_call_target="tpu_custom_call" | custom-call | tf_op jit(solution)/shard_map/tables/pallas_call | solution.py:174
  19.1 0.0 collective-permute-done.2.refs_3_
  19.1 0.0 collective-permute-done.1.refs_2_
  19.1 0.0 collective-permute-done.refs_1_
  19.2 4.8 %attend.1 = (f32[17,16,128]{2,1,0:T(8,128)S(1)}, bf16[17,16,128]{2,1,0:T(8,128)(2,1)S(1)}, bf16[17,16,128]{2,1,0:T(8,128)(2,1)S(1)}, bf16[17,16,128]{2,1,0:T(8,128)(2,1)S(1)}) custom-call(s32[145]{0:T(256)S(1)} %get-tuple-element.15.pos_t, s32[145]{0:T(256)S(1)} %get-tuple-element.16.page_t, s32[145]{0:T(256)S(1)} %get-tuple-element.17.fill_t, ...), custom_call_target="tpu_custom_call" | custom-call | tf_op jit(solution)/shard_map/attend/pallas_call | solution.py:196
  23.9 0.1 collective-permute-start.3
  24.0 2.4 %collective-permute-start.4 = (bf16[17,16,128]{2,1,0:T(8,128)(2,1)S(1)}, bf16[17,16,128]{2,1,0:T(8,128)(2,1)S(1)}, u32[]{:S(2)}, u32[]{:S(2)}) collective-permute-start(bf16[17,16,128]{2,1,0:T(8,128)(2,1)S(1)} %get-tuple-element.23), channel_id=1, source_target_pairs={{0,8},{4,12},{8,0},{12,4},{1,9},{5,13},{9,1},{13,5},{2,10},{6,14},... | collective-permute-start | bytes 208904 | tf_op jit(solution)/shard_map/ppermute | solution.py:213
  26.4 2.0 %collective-permute-start.5 = (bf16[17,16,128]{2,1,0:T(8,128)(2,1)S(1)}, bf16[17,16,128]{2,1,0:T(8,128)(2,1)S(1)}, u32[]{:S(2)}, u32[]{:S(2)}) collective-permute-start(bf16[17,16,128]{2,1,0:T(8,128)(2,1)S(1)} %get-tuple-element.24), channel_id=1, source_target_pairs={{0,12},{4,8},{8,4},{12,0},{1,13},{5,9},{9,5},{13,1},{2,14},{6,10},... | collective-permute-start | bytes 208904 | tf_op jit(solution)/shard_map/ppermute | solution.py:213
  28.4 0.0 collective-permute-done.3.refs_1_
  28.4 4.4 %collective-permute-done.4.refs_2_ = bf16[17,16,128]{2,1,0:T(8,128)(2,1)S(1)} collective-permute-done((bf16[17,16,128]{2,1,0:T(8,128)(2,1)S(1)}, bf16[17,16,128]{2,1,0:T(8,128)(2,1)S(1)}, u32[]{:S(2)}, u32[]{:S(2)}) %collective-permute-start.4) | collective-permute-done | bytes 69664 | tf_op jit(solution)/shard_map/ppermute | solution.py:213
  32.8 0.0 collective-permute-done.5.refs_3_
  32.8 0.8 %merge.1 = bf16[16,16,128]{2,1,0:T(8,128)(2,1)} custom-call(f32[17,16,128]{2,1,0:T(8,128)S(1)} %get-tuple-element.21.refs_0_, bf16[17,16,128]{2,1,0:T(8,128)(2,1)S(1)} %collective-permute-done.3.refs_1_, bf16[17,16,128]{2,1,0:T(8,128)(2,1)S(1)} %collective-permute-done.4.refs_2_, bf16[17,16,128]{2,1,0:T(8,128)(2,1)S(1)} %collective-permute-done.5.refs_3_), custom_call_target="tpu_custom_call" | custom-call | tf_op jit(solution)/shard_map/merge/pallas_call | solution.py:217
  (4 shorter events, 0.0 us)
Async XLA Ops:
  0.0 1.0 %copy-start = (bf16[16,64,128]{2,1,0:T(8,128)(2,1)S(1)}, bf16[16,64,128]{2,1,0:T(8,128)(2,1)}, u32[]{:S(2)}) copy-start(bf16[16,64,128]{2,1,0:T(8,128)(2,1)} %param.6) | copy-start | bytes 786436
  1.0 18.2 %collective-permute-start.2 = (bf16[16,16,128]{2,1,0:T(8,128)(2,1)S(1)}, bf16[16,16,128]{2,1,0:T(8,128)(2,1)S(1)}, u32[]{:S(2)}, u32[]{:S(2)}) collective-permute-start(bf16[16,16,128]{2,1,0:T(8,128)(2,1)S(1)} %constant_dynamic-slice_fusion.refs_0_), channel_id=1, source_target_pairs={{12,0},{8,4},{4,8},{0,12},{13,1},{9,5},{5,9},{1,13},{14,2},{10,6},... | collective-permute-start | bytes 196616 | tf_op jit(solution)/shard_map/ppermute | solution.py:167
  6.1 13.0 %collective-permute-start.1 = (bf16[16,16,128]{2,1,0:T(8,128)(2,1)S(1)}, bf16[16,16,128]{2,1,0:T(8,128)(2,1)S(1)}, u32[]{:S(2)}, u32[]{:S(2)}) collective-permute-start(bf16[16,16,128]{2,1,0:T(8,128)(2,1)S(1)} %constant_dynamic-slice_fusion.refs_0_), channel_id=1, source_target_pairs={{8,0},{12,4},{0,8},{4,12},{9,1},{13,5},{1,9},{5,13},{10,2},{14,6},... | collective-permute-start | bytes 196616 | tf_op jit(solution)/shard_map/ppermute | solution.py:167
  6.1 13.0 %collective-permute-start = (bf16[16,16,128]{2,1,0:T(8,128)(2,1)S(1)}, bf16[16,16,128]{2,1,0:T(8,128)(2,1)S(1)}, u32[]{:S(2)}, u32[]{:S(2)}) collective-permute-start(bf16[16,16,128]{2,1,0:T(8,128)(2,1)S(1)} %constant_dynamic-slice_fusion.refs_0_), channel_id=1, source_target_pairs={{4,0},{0,4},{12,8},{8,12},{5,1},{1,5},{13,9},{9,13},{6,2},{2,6},{1... | collective-permute-start | bytes 196616 | tf_op jit(solution)/shard_map/ppermute | solution.py:167
  6.8 2.2 %copy-start.1 = (bf16[128,2,64,128]{3,2,1,0:T(8,128)(2,1)S(1)}, bf16[128,2,64,128]{3,2,1,0:T(8,128)(2,1)}, u32[]{:S(2)}) copy-start(bf16[128,2,64,128]{3,2,1,0:T(8,128)(2,1)} %keys.1) | copy-start | bytes 12582916
  8.9 2.2 %copy-start.2 = (bf16[128,2,64,128]{3,2,1,0:T(8,128)(2,1)S(1)}, bf16[128,2,64,128]{3,2,1,0:T(8,128)(2,1)}, u32[]{:S(2)}) copy-start(bf16[128,2,64,128]{3,2,1,0:T(8,128)(2,1)} %values.1) | copy-start | bytes 12582916
  11.1 0.8 %copy-start.3 = (s32[64,128]{1,0:T(8,128)S(1)}, s32[64,128]{1,0:T(8,128)}, u32[]{:S(2)}) copy-start(s32[64,128]{1,0:T(8,128)} %owner.1) | copy-start | bytes 98308
  11.9 0.8 %copy-start.4 = (s32[64,128]{1,0:T(8,128)S(1)}, s32[64,128]{1,0:T(8,128)}, u32[]{:S(2)}) copy-start(s32[64,128]{1,0:T(8,128)} %local.1) | copy-start | bytes 98308
  12.6 0.7 %copy-start.5 = (s32[64]{0:T(128)S(1)}, s32[64]{0:T(128)}, u32[]{:S(2)}) copy-start(s32[64]{0:T(128)} %lens.1) | copy-start | bytes 772
  23.9 4.5 %collective-permute-start.3 = (bf16[17,16,128]{2,1,0:T(8,128)(2,1)S(1)}, bf16[17,16,128]{2,1,0:T(8,128)(2,1)S(1)}, u32[]{:S(2)}, u32[]{:S(2)}) collective-permute-start(bf16[17,16,128]{2,1,0:T(8,128)(2,1)S(1)} %get-tuple-element.22), channel_id=1, source_target_pairs={{0,4},{4,0},{8,12},{12,8},{1,5},{5,1},{9,13},{13,9},{2,6},{6,2},{1... | collective-permute-start | bytes 208904 | tf_op jit(solution)/shard_map/ppermute | solution.py:213
  24.0 8.8 %collective-permute-start.4 = (bf16[17,16,128]{2,1,0:T(8,128)(2,1)S(1)}, bf16[17,16,128]{2,1,0:T(8,128)(2,1)S(1)}, u32[]{:S(2)}, u32[]{:S(2)}) collective-permute-start(bf16[17,16,128]{2,1,0:T(8,128)(2,1)S(1)} %get-tuple-element.23), channel_id=1, source_target_pairs={{0,8},{4,12},{8,0},{12,4},{1,9},{5,13},{9,1},{13,5},{2,10},{6,14},... | collective-permute-start | bytes 208904 | tf_op jit(solution)/shard_map/ppermute | solution.py:213
  26.4 6.4 %collective-permute-start.5 = (bf16[17,16,128]{2,1,0:T(8,128)(2,1)S(1)}, bf16[17,16,128]{2,1,0:T(8,128)(2,1)S(1)}, u32[]{:S(2)}, u32[]{:S(2)}) collective-permute-start(bf16[17,16,128]{2,1,0:T(8,128)(2,1)S(1)} %get-tuple-element.24), channel_id=1, source_target_pairs={{0,12},{4,8},{8,4},{12,0},{1,13},{5,9},{9,5},{13,1},{2,14},{6,10},... | collective-permute-start | bytes 208904 | tf_op jit(solution)/shard_map/ppermute | solution.py:213

commit v2 on v1

--- a/solution.py
+++ b/solution.py
@@ -11,6 +11,7 @@
 HQ = 64
 KVH = 8
 GROUP = 16
+LOADS = 4
 
 score_shift = 8.0
 log2_e = math.log2(math.e)
@@ -35,15 +36,24 @@
 
 
 def table_kernel(
-    lens, owner, local, keys, values, pos_out, page_out, fill_out, count_out, keys_out, values_out,
-    sems, *, n, page_len
+    lens_in, owner_in, local_in, keys, values, pos_out, page_out, fill_out, count_out, keys_out,
+    values_out, lens, owner, local, sems, *, n, page_len
 ):
-    loads = [
-        pltpu.make_async_copy(keys, keys_out, sems.at[0]),
-        pltpu.make_async_copy(values, values_out, sems.at[1]),
+    small = [
+        pltpu.make_async_copy(lens_in, lens, sems.at[0]),
+        pltpu.make_async_copy(owner_in, owner, sems.at[1]),
+        pltpu.make_async_copy(local_in, local, sems.at[2]),
     ]
-    for load in loads:
+    cut = keys.shape[0] // LOADS
+    loads = []
+    for j in range(LOADS):
+        part = pl.ds(j * cut, cut)
+        loads.append(pltpu.make_async_copy(keys.at[part], keys_out.at[part], sems.at[3 + 2 * j]))
+        loads.append(pltpu.make_async_copy(values.at[part], values_out.at[part], sems.at[4 + 2 * j]))
+    for load in small + loads:
         load.start()
+    for load in small:
+        load.wait()
     rank = lax.axis_index("seq")
     seqs = owner.shape[0]
     own = seqs // n
@@ -171,6 +181,7 @@
     vmem = pl.BlockSpec(memory_space=pltpu.VMEM)
     table = jax.ShapeDtypeStruct((pool_pages + GROUP + 1,), jnp.int32)
     hbm = pl.BlockSpec(memory_space=pltpu.HBM)
+    held = (seq_lengths, page_owner, page_local, key_pages, value_pages)
     *tables, keys, values = pl.pallas_call(
         functools.partial(table_kernel, n=n, page_len=page_len),
         out_shape=[
@@ -181,12 +192,17 @@
             jax.ShapeDtypeStruct(key_pages.shape, key_pages.dtype),
             jax.ShapeDtypeStruct(value_pages.shape, value_pages.dtype),
         ],
-        in_specs=[smem] * 3 + [hbm] * 2,
+        in_specs=[hbm] * 5,
         out_specs=[smem] * 4 + [vmem] * 2,
-        scratch_shapes=[pltpu.SemaphoreType.DMA((2,))],
+        scratch_shapes=[
+            pltpu.SMEM(seq_lengths.shape, jnp.int32),
+            pltpu.SMEM(page_owner.shape, jnp.int32),
+            pltpu.SMEM(page_local.shape, jnp.int32),
+            pltpu.SemaphoreType.DMA((3 + 2 * LOADS,)),
+        ],
         compiler_params=pltpu.CompilerParams(vmem_limit_bytes=1024 * 1024),
         name="tables",
-    )(seq_lengths, page_owner, page_local, key_pages, value_pages)
+    )(*[pltpu.with_memory_space_constraint(x, pltpu.HBM) for x in held])
     sent = jax.ShapeDtypeStruct((own + 1, heads, head_dim), jnp.bfloat16)
     kept = jax.ShapeDtypeStruct((own + 1, heads, head_dim), jnp.float32)
     if direct(n):

time: 34.3 us -> 27.5 us (0.80); the launches traced: 33.6 us -> 27.8 us
  local copies, waits for them, and re-layouts: 7.5 us -> 0.96 us
  waiting for transfers between devices: 4.39 us -> 6.04 us
  Pallas kernels: 11.4 us -> 10.5 us
    unnamed x12 -> x2, local copies, waits for them, and re-layouts: 7.49 us -> 0.95 us
    ppermute x3, waiting for transfers between devices: 4.38 us -> 6.03 us  [body(): pieces.append(lax.ppermute(partial[s], 'seq', pairs))]
    pallas_call x1, Pallas kernels: 4.78 us -> 4.23 us  [body(): pl.pallas_call(functools.partial(attend_kernel, n=n, parts=len(parts), kv...]
    pallas_call x1, Pallas kernels: 5.82 us -> 5.41 us  [body(): pl.pallas_call(functools.partial(table_kernel, n=n, page_len=page_len), o...]
  transfers between devices with their start and end apart: 6 -> 6, of which waited for: 1 -> 3; matrix products, arithmetic and copies ran while one was open for 0% -> 0% of each run, Pallas kernels for 17% -> 19%
where the time goes in v2:
time: 27.5 us; the launch traced here: 27.8 us
  Pallas kernels  10.5 us (38%)
  starting transfers between devices  10.2 us (37%)
  waiting for transfers between devices  6.04 us (22%)
  local copies, waits for them, and re-layouts  0.96 us (3%)
    ppermute x3, waiting for transfers between devices, body(): pieces.append(lax.ppermute(partial[s], 'seq', pairs))  6.03 us
    ppermute x3, starting transfers between devices, body(): lax.ppermute(mine, 'seq', fetch_pairs(n, s))  5.78 us
    pallas_call x1, Pallas kernels, body(): pl.pallas_call(functools.partial(table_kernel, n=n, page_len=page_len), o...  5.41 us
    ppermute x3, starting transfers between devices, body(): pieces.append(lax.ppermute(partial[s], 'seq', pairs))  4.44 us
    pallas_call x1, Pallas kernels, body(): pl.pallas_call(functools.partial(attend_kernel, n=n, parts=len(parts), kv...  4.23 us
    unnamed x2, local copies, waits for them, and re-layouts  0.95 us
    pallas_call x1, Pallas kernels, body(): pl.pallas_call(functools.partial(merge_kernel, own=own), out_shape=jax.Sh...  0.83 us
  transfers between devices with their start and end apart: 6, of which 3 were waited for; matrix products, arithmetic and copies ran while one was open for 0% of the time, Pallas kernels for 19%

profile of v2, /device:TPU:0, one launch (start us, length us, event | category | flops | bytes accessed | tf_op | source)
XLA Modules:
  0.0 27.8 jit_solution(8074068705507482303)
XLA Ops:
  0.0 0.0 copy-start
  0.0 0.9 %copy-done = bf16[16,64,128]{2,1,0:T(8,128)(2,1)S(1)} copy-done((bf16[16,64,128]{2,1,0:T(8,128)(2,1)S(1)}, bf16[16,64,128]{2,1,0:T(8,128)(2,1)}, u32[]{:S(2)}) %copy-start) | copy-done | bytes 262168
  1.0 5.1 %collective-permute-start.2 = (bf16[16,16,128]{2,1,0:T(8,128)(2,1)S(1)}, bf16[16,16,128]{2,1,0:T(8,128)(2,1)S(1)}, u32[]{:S(2)}, u32[]{:S(2)}) collective-permute-start(bf16[16,16,128]{2,1,0:T(8,128)(2,1)S(1)} %constant_dynamic-slice_fusion.refs_0_), channel_id=1, source_target_pairs={{12,0},{8,4},{4,8},{0,12},{13,1},{9,5},{5,9},{1,13},{14,2},{10,6},... | collective-permute-start | bytes 196616 | tf_op jit(solution)/shard_map/ppermute | solution.py:177
  6.1 0.0 collective-permute-start.1
  6.1 0.6 %collective-permute-start = (bf16[16,16,128]{2,1,0:T(8,128)(2,1)S(1)}, bf16[16,16,128]{2,1,0:T(8,128)(2,1)S(1)}, u32[]{:S(2)}, u32[]{:S(2)}) collective-permute-start(bf16[16,16,128]{2,1,0:T(8,128)(2,1)S(1)} %constant_dynamic-slice_fusion.refs_0_), channel_id=1, source_target_pairs={{4,0},{0,4},{12,8},{8,12},{5,1},{1,5},{13,9},{9,13},{6,2},{2,6},{1... | collective-permute-start | bytes 196616 | tf_op jit(solution)/shard_map/ppermute | solution.py:177
  6.8 5.4 %tables.1 = (s32[145]{0:T(256)S(1)}, s32[145]{0:T(256)S(1)}, s32[145]{0:T(256)S(1)}, s32[1]{0:T(128)}, bf16[128,2,64,128]{3,2,1,0:T(8,128)(2,1)S(1)}, /*index=5*/bf16[128,2,64,128]{3,2,1,0:T(8,128)(2,1)S(1)}) custom-call(s32[64]{0:T(128)} %lens_in.1, s32[64,128]{1,0:T(8,128)} %owner_in.1, s32[64,128]{1,0:T(8,128)} %local_in.1, ...), custom_call_target="tpu_custom_call" | custom-call | tf_op jit(solution)/shard_map/tables/pallas_call | solution.py:185
  12.2 0.0 collective-permute-done.2.refs_3_
  12.2 0.0 collective-permute-done.1.refs_2_
  12.2 0.0 collective-permute-done.refs_1_
  12.2 4.2 %attend.1 = (f32[17,16,128]{2,1,0:T(8,128)S(1)}, bf16[17,16,128]{2,1,0:T(8,128)(2,1)S(1)}, bf16[17,16,128]{2,1,0:T(8,128)(2,1)S(1)}, bf16[17,16,128]{2,1,0:T(8,128)(2,1)S(1)}) custom-call(s32[145]{0:T(256)S(1)} %get-tuple-element.15.pos_t, s32[145]{0:T(256)S(1)} %get-tuple-element.16.page_t, s32[145]{0:T(256)S(1)} %get-tuple-element.17.fill_t, ...), custom_call_target="tpu_custom_call" | custom-call | tf_op jit(solution)/shard_map/attend/pallas_call | solution.py:212
  16.4 0.1 collective-permute-start.3
  16.5 4.3 %collective-permute-start.4 = (bf16[17,16,128]{2,1,0:T(8,128)(2,1)S(1)}, bf16[17,16,128]{2,1,0:T(8,128)(2,1)S(1)}, u32[]{:S(2)}, u32[]{:S(2)}) collective-permute-start(bf16[17,16,128]{2,1,0:T(8,128)(2,1)S(1)} %get-tuple-element.23), channel_id=1, source_target_pairs={{0,8},{4,12},{8,0},{12,4},{1,9},{5,13},{9,1},{13,5},{2,10},{6,14},... | collective-permute-start | bytes 208904 | tf_op jit(solution)/shard_map/ppermute | solution.py:229
  20.8 0.1 collective-permute-start.5
  20.9 0.5 %collective-permute-done.3.refs_1_ = bf16[17,16,128]{2,1,0:T(8,128)(2,1)S(1)} collective-permute-done((bf16[17,16,128]{2,1,0:T(8,128)(2,1)S(1)}, bf16[17,16,128]{2,1,0:T(8,128)(2,1)S(1)}, u32[]{:S(2)}, u32[]{:S(2)}) %collective-permute-start.3) | collective-permute-done | bytes 69664 | tf_op jit(solution)/shard_map/ppermute | solution.py:229
  21.4 3.5 %collective-permute-done.4.refs_2_ = bf16[17,16,128]{2,1,0:T(8,128)(2,1)S(1)} collective-permute-done((bf16[17,16,128]{2,1,0:T(8,128)(2,1)S(1)}, bf16[17,16,128]{2,1,0:T(8,128)(2,1)S(1)}, u32[]{:S(2)}, u32[]{:S(2)}) %collective-permute-start.4) | collective-permute-done | bytes 69664 | tf_op jit(solution)/shard_map/ppermute | solution.py:229
  24.9 2.1 %collective-permute-done.5.refs_3_ = bf16[17,16,128]{2,1,0:T(8,128)(2,1)S(1)} collective-permute-done((bf16[17,16,128]{2,1,0:T(8,128)(2,1)S(1)}, bf16[17,16,128]{2,1,0:T(8,128)(2,1)S(1)}, u32[]{:S(2)}, u32[]{:S(2)}) %collective-permute-start.5) | collective-permute-done | bytes 69664 | tf_op jit(solution)/shard_map/ppermute | solution.py:229
  26.9 0.8 %merge.1 = bf16[16,16,128]{2,1,0:T(8,128)(2,1)} custom-call(f32[17,16,128]{2,1,0:T(8,128)S(1)} %get-tuple-element.21.refs_0_, bf16[17,16,128]{2,1,0:T(8,128)(2,1)S(1)} %collective-permute-done.3.refs_1_, bf16[17,16,128]{2,1,0:T(8,128)(2,1)S(1)} %collective-permute-done.4.refs_2_, bf16[17,16,128]{2,1,0:T(8,128)(2,1)S(1)} %collective-permute-done.5.refs_3_), custom_call_target="tpu_custom_call" | custom-call | tf_op jit(solution)/shard_map/merge/pallas_call | solution.py:233
  (1 shorter events, 0.0 us)
Async XLA Ops:
  0.0 1.0 %copy-start = (bf16[16,64,128]{2,1,0:T(8,128)(2,1)S(1)}, bf16[16,64,128]{2,1,0:T(8,128)(2,1)}, u32[]{:S(2)}) copy-start(bf16[16,64,128]{2,1,0:T(8,128)(2,1)} %param.6) | copy-start | bytes 786436
  1.0 11.2 %collective-permute-start.2 = (bf16[16,16,128]{2,1,0:T(8,128)(2,1)S(1)}, bf16[16,16,128]{2,1,0:T(8,128)(2,1)S(1)}, u32[]{:S(2)}, u32[]{:S(2)}) collective-permute-start(bf16[16,16,128]{2,1,0:T(8,128)(2,1)S(1)} %constant_dynamic-slice_fusion.refs_0_), channel_id=1, source_target_pairs={{12,0},{8,4},{4,8},{0,12},{13,1},{9,5},{5,9},{1,13},{14,2},{10,6},... | collective-permute-start | bytes 196616 | tf_op jit(solution)/shard_map/ppermute | solution.py:177
  6.1 6.1 %collective-permute-start.1 = (bf16[16,16,128]{2,1,0:T(8,128)(2,1)S(1)}, bf16[16,16,128]{2,1,0:T(8,128)(2,1)S(1)}, u32[]{:S(2)}, u32[]{:S(2)}) collective-permute-start(bf16[16,16,128]{2,1,0:T(8,128)(2,1)S(1)} %constant_dynamic-slice_fusion.refs_0_), channel_id=1, source_target_pairs={{8,0},{12,4},{0,8},{4,12},{9,1},{13,5},{1,9},{5,13},{10,2},{14,6},... | collective-permute-start | bytes 196616 | tf_op jit(solution)/shard_map/ppermute | solution.py:177
  6.1 6.1 %collective-permute-start = (bf16[16,16,128]{2,1,0:T(8,128)(2,1)S(1)}, bf16[16,16,128]{2,1,0:T(8,128)(2,1)S(1)}, u32[]{:S(2)}, u32[]{:S(2)}) collective-permute-start(bf16[16,16,128]{2,1,0:T(8,128)(2,1)S(1)} %constant_dynamic-slice_fusion.refs_0_), channel_id=1, source_target_pairs={{4,0},{0,4},{12,8},{8,12},{5,1},{1,5},{13,9},{9,13},{6,2},{2,6},{1... | collective-permute-start | bytes 196616 | tf_op jit(solution)/shard_map/ppermute | solution.py:177
  16.4 4.9 %collective-permute-start.3 = (bf16[17,16,128]{2,1,0:T(8,128)(2,1)S(1)}, bf16[17,16,128]{2,1,0:T(8,128)(2,1)S(1)}, u32[]{:S(2)}, u32[]{:S(2)}) collective-permute-start(bf16[17,16,128]{2,1,0:T(8,128)(2,1)S(1)} %get-tuple-element.22), channel_id=1, source_target_pairs={{0,4},{4,0},{8,12},{12,8},{1,5},{5,1},{9,13},{13,9},{2,6},{6,2},{1... | collective-permute-start | bytes 208904 | tf_op jit(solution)/shard_map/ppermute | solution.py:229
  16.5 8.3 %collective-permute-start.4 = (bf16[17,16,128]{2,1,0:T(8,128)(2,1)S(1)}, bf16[17,16,128]{2,1,0:T(8,128)(2,1)S(1)}, u32[]{:S(2)}, u32[]{:S(2)}) collective-permute-start(bf16[17,16,128]{2,1,0:T(8,128)(2,1)S(1)} %get-tuple-element.23), channel_id=1, source_target_pairs={{0,8},{4,12},{8,0},{12,4},{1,9},{5,13},{9,1},{13,5},{2,10},{6,14},... | collective-permute-start | bytes 208904 | tf_op jit(solution)/shard_map/ppermute | solution.py:229
  20.8 6.1 %collective-permute-start.5 = (bf16[17,16,128]{2,1,0:T(8,128)(2,1)S(1)}, bf16[17,16,128]{2,1,0:T(8,128)(2,1)S(1)}, u32[]{:S(2)}, u32[]{:S(2)}) collective-permute-start(bf16[17,16,128]{2,1,0:T(8,128)(2,1)S(1)} %get-tuple-element.24), channel_id=1, source_target_pairs={{0,12},{4,8},{8,4},{12,0},{1,13},{5,9},{9,5},{13,1},{2,14},{6,10},... | collective-permute-start | bytes 208904 | tf_op jit(solution)/shard_map/ppermute | solution.py:229
